TPU v7x, 32 devices: a whole 2x2x4 slice. The times are simulated.
32 devices in a mesh: expert: 4 (over z), shard: 8 (over y, x, core).
Axes of the slice: x: 2, y: 2, z: 4, core: 2. Of those that a mesh axis runs over, the one named last changes fastest.
Arguments:
- master_gate: float32 [64, 2048, 1408], P('expert', 'shard'), may hold values from -0.1875 to 0.1875
- master_up: float32 [64, 2048, 1408], P('expert', 'shard'), may hold values from -0.1875 to 0.1875
- router_weight: float32 [2048, 64], P('shard', 'expert'), may hold values from -0.125 to 0.125
- router_gain: float32 [2048], P('shard'), may hold values from 0.25 to 1.75
Outputs:
- final_gate: bfloat16 [64, 2048, 1408], P('expert', None, 'shard')
- final_up: bfloat16 [64, 2048, 1408], P('expert', None, 'shard')
- scale_gate: float32 [64, 1408], P('expert', 'shard')
- scale_up: float32 [64, 1408], P('expert', 'shard')
- serve_router: bfloat16 [2048, 64], replicated
All inputs are finite; a program needn't handle non-finite values.
Results may differ from a plain program's by a relative error of at most 0.001.
Values may be sent and summed in bfloat16 or wider, within the bound.
A program may use at most 192 MiB of HBM per device.

v0:
```python
import jax
import jax.numpy as jnp
from jax import lax
from jax.sharding import PartitionSpec as P


def local(master_gate, master_up, router_weight, router_gain):
    total_gate, total_up = lax.psum(
        (jnp.sum(master_gate * master_gate, axis=1), jnp.sum(master_up * master_up, axis=1)),
        "shard",
    )
    scale_gate = jnp.sqrt(total_gate)
    scale_up = jnp.sqrt(total_up)
    narrow_gate, narrow_up = (
        (master_gate / jnp.expand_dims(scale_gate, 1)).astype(jnp.bfloat16),
        (master_up / jnp.expand_dims(scale_up, 1)).astype(jnp.bfloat16),
    )
    final_gate, final_up = (
        lax.all_to_all(narrow_gate, "shard", split_axis=2, concat_axis=1, tiled=True),
        lax.all_to_all(narrow_up, "shard", split_axis=2, concat_axis=1, tiled=True),
    )
    scale_gate = lax.dynamic_slice_in_dim(
        scale_gate, lax.axis_index("shard") * final_gate.shape[2], final_gate.shape[2], axis=1
    )
    scale_up = lax.dynamic_slice_in_dim(
        scale_up, lax.axis_index("shard") * final_up.shape[2], final_up.shape[2], axis=1
    )
    part_router = (router_weight * router_gain[:, None]).astype(jnp.bfloat16)
    row_router = lax.all_gather(part_router, "shard", axis=0, tiled=True)
    serve_router = lax.all_gather(row_router, "expert", axis=1, tiled=True)
    return (final_gate, final_up, scale_gate, scale_up, serve_router)


def solution(mesh):
    in_specs = (
        P("expert", "shard", None),
        P("expert", "shard", None),
        P("shard", "expert"),
        P("shard"),
    )
    out_specs = (
        P("expert", None, "shard"),
        P("expert", None, "shard"),
        P("expert", "shard"),
        P("expert", "shard"),
        P(),
    )
    return jax.shard_map(local, mesh=mesh, in_specs=in_specs, out_specs=out_specs, check_vma=False)
```

profile of v0, /device:TPU:1, one launch (start us, length us, event | category | flops | bytes accessed | tf_op | source)
XLA Modules:
  0.0 443.1 jit_solution(13781813590717320649)
XLA Ops:
  7.2 0.0 all-reduce.3.cloned.1.call-start
  7.2 15.8 %multiply_reduce_fusion = (f32[16,1408]{1,0:T(8,128)}, f32[16,1408]{1,0:T(8,128)}) fusion(f32[16,256,1408]{2,1,0:T(8,128)} %param.5, f32[16,256,1408]{2,1,0:T(8,128)} %param.4), kind=kLoop, calls=%fused_computation.1 | loop fusion | flops 23023616 | bytes 46317568 | tf_op jit(solution)/shard_map/reduce_sum | solution.py:9
  23.0 0.0 all-reduce.3.cloned.1.call-update
  23.1 23.7 %copy.22 = f32[16,256,1408]{1,0,2:T(8,128)} copy(f32[16,256,1408]{2,1,0:T(8,128)} %param.5) | data formatting | bytes 46137344 | tf_op args[1]
  46.7 31.6 %all-reduce.3.cloned.1.call-done = (f32[16,1408]{1,0:T(8,128)}, f32[16,1408]{1,0:T(8,128)}) async-done(((f32[16,1408]{1,0:T(8,128)}, f32[16,1408]{1,0:T(8,128)}), (f32[16,1408]{1,0:T(8,128)}, f32[16,1408]{1,0:T(8,128)})) %all-reduce.3.cloned.1.call-update) | async-done | bytes 180240 | tf_op jit(solution)/shard_map/psum | solution.py:8
  78.3 0.9 sqrt.7
  79.3 0.3 copy.21
  79.5 14.2 %divide_convert_fusion = bf16[16,256,1408]{1,0,2:T(8,128)(2,1)} fusion(f32[16,256,1408]{1,0,2:T(8,128)} %copy.22, f32[16,1408]{0,1:T(8,128)S(1)} %copy.21), kind=kLoop, calls=%fused_computation | loop fusion | flops 11534336 | bytes 34693120 | tf_op jit(solution)/shard_map/convert_element_type | solution.py:16
  93.7 5.8 %all-to-all-start.1 = ((bf16[16,256,1408]{1,0,2:T(8,128)(2,1)}), bf16[16,256,1408]{1,0,2:T(8,128)(2,1)}, u32[]{:S(2)}, u32[]{:S(2)}) async-start(bf16[16,256,1408]{1,0,2:T(8,128)(2,1)} %divide_convert_fusion), calls=%async_computation.1 | async-start | bytes 23068672 | tf_op jit(solution)/shard_map/all_to_all | solution.py:20
  99.6 0.0 copy-start
  99.6 23.7 %copy.18 = f32[16,256,1408]{1,0,2:T(8,128)} copy(f32[16,256,1408]{2,1,0:T(8,128)} %param.4) | data formatting | bytes 46137344 | tf_op args[0]
  123.3 0.0 copy-done
  123.3 0.3 copy.17
  123.6 0.0 copy-start.1
  123.6 0.0 copy-start.2
  123.6 14.2 %divide_convert_fusion.1 = bf16[16,256,1408]{1,0,2:T(8,128)(2,1)} fusion(f32[16,256,1408]{1,0,2:T(8,128)} %copy.18, f32[16,1408]{0,1:T(8,128)S(1)} %copy.17), kind=kLoop, calls=%fused_computation.2 | loop fusion | flops 11534336 | bytes 34693120 | tf_op jit(solution)/shard_map/convert_element_type | solution.py:15
  137.8 86.0 %all-to-all-done.1 = bf16[16,256,1408]{1,0,2:T(8,128)(2,1)} async-done(((bf16[16,256,1408]{1,0,2:T(8,128)(2,1)}), bf16[16,256,1408]{1,0,2:T(8,128)(2,1)}, u32[]{:S(2)}, u32[]{:S(2)}) %all-to-all-start.1) | async-done | bytes 11534368 | tf_op jit(solution)/shard_map/all_to_all | solution.py:20
  223.8 8.8 %all-to-all-start = ((bf16[16,256,1408]{1,0,2:T(8,128)(2,1)}), bf16[16,256,1408]{1,0,2:T(8,128)(2,1)}, u32[]{:S(2)}, u32[]{:S(2)}) async-start(bf16[16,256,1408]{1,0,2:T(8,128)(2,1)} %divide_convert_fusion.1), calls=%async_computation | async-start | bytes 23068672 | tf_op jit(solution)/shard_map/all_to_all | solution.py:19
  232.6 0.0 copy-done.1
  232.6 0.0 copy-done.2
  232.6 130.9 %all_gather.6 = bf16[2048,16]{0,1:T(8,128)(2,1)S(1)} all-gather(bf16[256,16]{0,1:T(8,128)(2,1)S(1)} %multiply_convert_fusion), channel_id=1, replica_groups=mesh['expert'=4,'shard'=8] {'shard'}, dimensions={0}, use_global_device_ids=true | all-gather | bytes 73728 | tf_op jit(solution)/shard_map/all_gather | solution.py:29
  363.5 12.1 %all_gather.7 = bf16[2048,64]{0,1:T(8,128)(2,1)S(1)} all-gather(bf16[2048,16]{0,1:T(8,128)(2,1)S(1)} %all_gather.6), channel_id=1, replica_groups=mesh['expert'=4,'shard'=8] {'expert'}, dimensions={1}, use_global_device_ids=true | all-gather | bytes 327680 | tf_op jit(solution)/shard_map/all_gather | solution.py:30
  375.6 0.7 constant_dynamic-slice_fusion
  376.2 0.7 constant_dynamic-slice_fusion.1
  376.9 11.4 %copy.24 = bf16[16,8,256,176]{2,1,3,0:T(8,128)(2,1)} copy(bf16[16,8,256,176]{2,0,3,1:T(8,128)(2,1)} %bitcast.5) | data formatting | bytes 23068672 | tf_op jit(solution)/shard_map/all_to_all | solution.py:20
  388.3 18.0 %all_to_all.33 = bf16[16,2048,176]{1,2,0:T(8,128)(2,1)} reshape(bf16[16,8,256,176]{2,1,3,0:T(8,128)(2,1)} %copy.24) | data formatting | bytes 23068672 | tf_op jit(solution)/shard_map/all_to_all | solution.py:20
  406.2 0.0 all-to-all-done
  406.2 11.4 %copy.20 = bf16[16,8,256,176]{2,1,3,0:T(8,128)(2,1)} copy(bf16[16,8,256,176]{2,0,3,1:T(8,128)(2,1)} %bitcast.2) | data formatting | bytes 23068672 | tf_op jit(solution)/shard_map/all_to_all | solution.py:19
  417.6 18.0 %all_to_all.29 = bf16[16,2048,176]{1,2,0:T(8,128)(2,1)} reshape(bf16[16,8,256,176]{2,1,3,0:T(8,128)(2,1)} %copy.20) | data formatting | bytes 23068672 | tf_op jit(solution)/shard_map/all_to_all | solution.py:19
  435.6 0.7 copy.30
  (2 shorter events, 0.0 us)
Async XLA Ops:
  7.2 71.2 %all-reduce.3.cloned.1.call-start = ((), (), s32[]{:S(2)}) async-start(), calls=%async_computation.2 | async-start | bytes 360448 | tf_op jit(solution)/shard_map/psum | solution.py:8
  93.7 130.1 %all-to-all-start.1 = ((bf16[16,256,1408]{1,0,2:T(8,128)(2,1)}), bf16[16,256,1408]{1,0,2:T(8,128)(2,1)}, u32[]{:S(2)}, u32[]{:S(2)}) async-start(bf16[16,256,1408]{1,0,2:T(8,128)(2,1)} %divide_convert_fusion), calls=%async_computation.1 | async-start | bytes 23068672 | tf_op jit(solution)/shard_map/all_to_all | solution.py:20
  99.6 23.7 %copy-start = (f32[16,1408]{1,0:T(8,128)S(1)}, f32[16,1408]{1,0:T(8,128)}, u32[]{:S(2)}) copy-start(f32[16,1408]{1,0:T(8,128)} %get-tuple-element.5) | copy-start | bytes 270340
  123.6 109.0 %copy-start.1 = (f32[256,16]{0,1:T(8,128)S(1)}, f32[256,16]{0,1:T(8,128)}, u32[]{:S(2)}) copy-start(f32[256,16]{0,1:T(8,128)} %param.6) | copy-start | bytes 49156
  123.6 109.0 %copy-start.2 = (f32[256]{0:T(256)S(1)}, f32[256]{0:T(256)}, u32[]{:S(2)}) copy-start(f32[256]{0:T(256)} %param.7) | copy-start | bytes 3076
  223.8 182.4 %all-to-all-start = ((bf16[16,256,1408]{1,0,2:T(8,128)(2,1)}), bf16[16,256,1408]{1,0,2:T(8,128)(2,1)}, u32[]{:S(2)}, u32[]{:S(2)}) async-start(bf16[16,256,1408]{1,0,2:T(8,128)(2,1)} %divide_convert_fusion.1), calls=%async_computation | async-start | bytes 23068672 | tf_op jit(solution)/shard_map/all_to_all | solution.py:19
Sparse Core Ops, SparseCore 0:
  23.2 55.1 all-reduce.2
where the time goes:
time: 447 us; the launch traced here: 443 us
  blocking collectives  143 us (32%)
  waiting for transfers between devices  118 us (26%)
  local copies, waits for them, and re-layouts  110 us (25%)
  other arithmetic  44.3 us (10%)
  starting transfers between devices  14.6 us (3%)
  between operations  14.1 us (3%)
    all_gather x1, blocking collectives, local(): row_router = lax.all_gather(part_router, 'shard', axis=0, tiled=True)  131 us
    all_to_all x1, waiting for transfers between devices, local(): lax.all_to_all(narrow_up, 'shard', split_axis=2, concat_axis=1, tiled=True)  86 us
    unnamed x9, local copies, waits for them, and re-layouts  48.1 us
    psum x1, waiting for transfers between devices, local(): lax.psum((jnp.sum(master_gate * master_gate, axis=1), jnp.sum(master_up *...  31.6 us
    all_to_all x2, local copies, waits for them, and re-layouts, local(): lax.all_to_all(narrow_gate, 'shard', split_axis=2, concat_axis=1, tiled=T...  29.3 us
    all_to_all x2, local copies, waits for them, and re-layouts, local(): lax.all_to_all(narrow_up, 'shard', split_axis=2, concat_axis=1, tiled=True)  29.3 us
    reduce_sum x1, other arithmetic, local(): jnp.sum(master_up * master_up, axis=1)  15.8 us
    convert_element_type x1, other arithmetic, local(): (master_up / jnp.expand_dims(scale_up, 1)).astype(jnp.bfloat16)  14.2 us
  transfers between devices with their start and end apart: 3, of which 2 were waited for; matrix products, arithmetic and copies ran while one was open for 17% of the time, Pallas kernels for 0%

commit v1 on v0

--- a/solution.py
+++ b/solution.py
@@ -1,10 +1,19 @@
+import functools
+
 import jax
 import jax.numpy as jnp
 from jax import lax
+from jax.experimental import pallas as pl
+from jax.experimental.pallas import tpu as pltpu
 from jax.sharding import PartitionSpec as P
 
-
-def local(master_gate, master_up, router_weight, router_gain):
+GROUP = 8
+SLOTS = 16
+LANES = 128
+VMEM_LIMIT = 62914560
+
+
+def plain(master_gate, master_up, router_weight, router_gain):
     total_gate, total_up = lax.psum(
         (jnp.sum(master_gate * master_gate, axis=1), jnp.sum(master_up * master_up, axis=1)),
         "shard",
@@ -31,7 +40,241 @@
     return (final_gate, final_up, scale_gate, scale_up, serve_router)
 
 
+def kernel(n, nz, gate, up, weight, gain, out, scale_out, router_out,
+           buf, slots, part, got, inverse, column,
+           load_sem, send_sem, own_sem, recv_sem, part_send, part_recv,
+           first_send, first_recv, second_send, second_recv, router_own):
+    me = lax.axis_index("shard")
+    mez = lax.axis_index("expert")
+    experts, rows, width = gate.shape
+    slabs = 2 * experts
+    groups = slabs // GROUP
+    narrow = width // n
+    router_rows = weight.shape[0]
+
+    def load(source, e, k):
+        return pltpu.make_async_copy(source.at[e], buf.at[k], load_sem.at[k])
+
+    def start_gate(e, _):
+        load(gate, e, e).start()
+        return 0
+
+    def start_up(e, _):
+        load(up, e, experts + e).start()
+        return 0
+
+    lax.fori_loop(0, experts, start_gate, 0)
+    lax.fori_loop(0, experts, start_up, 0)
+
+    barrier = pltpu.get_barrier_semaphore()
+    for r in range(1, n):
+        pl.semaphore_signal(barrier, inc=1, device_id={"shard": lax.rem(me + r, n)},
+                            device_id_type=pl.DeviceIdType.MESH)
+    for r in range(1, nz):
+        pl.semaphore_signal(barrier, inc=1, device_id={"expert": lax.rem(mez + r, nz)},
+                            device_id_type=pl.DeviceIdType.MESH)
+
+    my_rows = pl.ds(pl.multiple_of(mez * router_rows, router_rows), router_rows)
+    my_lanes = pl.ds(pl.multiple_of(me * rows, rows), rows)
+    column[my_rows, :] = (weight[...] * gain[...]).astype(jnp.bfloat16)
+    pl.semaphore_wait(barrier, n - 1 + nz - 1)
+
+    def sums(g):
+        def one(i, _):
+            k = g * GROUP + i
+            load(gate, 0, k).wait()
+            x = buf[k]
+            part[g, pl.ds(i, 1), :] = jnp.sum(x * x, axis=0, keepdims=True)
+            return 0
+        lax.fori_loop(0, GROUP, one, 0)
+
+    def part_copy(g, r):
+        return pltpu.make_async_remote_copy(
+            src_ref=part.at[g], dst_ref=got.at[g, r - 1],
+            send_sem=part_send.at[g, r - 1], recv_sem=part_recv.at[g, r - 1],
+            device_id={"shard": lax.rem(me + r, n)}, device_id_type=pl.DeviceIdType.MESH)
+
+    def send_part(g):
+        for r in range(1, n):
+            part_copy(g, r).start()
+
+    def first_copy(r):
+        return pltpu.make_async_remote_copy(
+            src_ref=column.at[my_rows, :], dst_ref=column.at[my_rows, :],
+            send_sem=first_send.at[r - 1], recv_sem=first_recv.at[r - 1],
+            device_id={"expert": lax.rem(mez + r, nz)}, device_id_type=pl.DeviceIdType.MESH)
+
+    def second_copy(r):
+        return pltpu.make_async_remote_copy(
+            src_ref=column, dst_ref=router_out.at[:, my_lanes],
+            send_sem=second_send.at[r - 1], recv_sem=second_recv.at[r - 1],
+            device_id={"shard": lax.rem(me + r, n)}, device_id_type=pl.DeviceIdType.MESH)
+
+    own_router = pltpu.make_async_copy(column, router_out.at[:, my_lanes], router_own)
+
+    def slab_copy(k, r):
+        target = lax.rem(me + r, n)
+        s = k % SLOTS
+        return pltpu.make_async_remote_copy(
+            src_ref=slots.at[s, pl.ds(pl.multiple_of(target * narrow, 16), narrow), :],
+            dst_ref=out.at[k, :, my_lanes],
+            send_sem=send_sem.at[s, r - 1], recv_sem=recv_sem.at[r - 1],
+            device_id={"shard": target}, device_id_type=pl.DeviceIdType.MESH)
+
+    def own_copy(k):
+        s = k % SLOTS
+        return pltpu.make_async_copy(
+            slots.at[s, pl.ds(pl.multiple_of(me * narrow, 16), narrow), :],
+            out.at[k, :, my_lanes], own_sem.at[s])
+
+    def send_slab(k):
+        for r in range(1, n):
+            slab_copy(k, r).start()
+        own_copy(k).start()
+
+    def wait_slab(k):
+        for r in range(1, n):
+            slab_copy(k, r).wait_send()
+        own_copy(k).wait()
+
+    def narrow_slab(g, i):
+        k = g * GROUP + i
+
+        @pl.when(k >= SLOTS)
+        def _():
+            wait_slab(k - SLOTS)
+
+        s = k % SLOTS
+
+        def tile(j, _):
+            lanes = pl.ds(pl.multiple_of(j * LANES, LANES), LANES)
+            y = buf[k, :, lanes] * inverse[j, pl.ds(k, 1), :]
+            slots[s, lanes, :] = y.T.astype(jnp.bfloat16)
+            return 0
+
+        lax.fori_loop(0, width // LANES, tile, 0)
+
+    for g in range(groups):
+        sums(g)
+        if g == 0:
+            for r in range(1, nz):
+                first_copy(r).start()
+        else:
+            send_part(g - 1)
+        if g == 1:
+            for r in range(1, nz):
+                first_copy(r).wait()
+            for r in range(1, n):
+                second_copy(r).start()
+            own_router.start()
+
+    for g in range(groups):
+        for r in range(1, n):
+            part_copy(g, r).wait_recv()
+        total = part[g]
+        for r in range(1, n):
+            total = total + got[g, r - 1]
+        scale = jnp.sqrt(total)
+        scale_out[g * GROUP:(g + 1) * GROUP, :] = scale
+        reciprocal = 1.0 / scale
+        for j in range(width // LANES):
+            inverse[j, g * GROUP:(g + 1) * GROUP, :] = reciprocal[:, j * LANES:(j + 1) * LANES]
+
+        def step(i, _):
+            narrow_slab(g, i)
+            k = g * GROUP + i
+
+            @pl.when(k > 0)
+            def _():
+                send_slab(k - 1)
+
+            if g == 0:
+                @pl.when(k == 0)
+                def _():
+                    send_part(groups - 1)
+            return 0
+
+        lax.fori_loop(0, GROUP, step, 0)
+
+    for r in range(1, n):
+        second_copy(r).wait_send()
+    for g in range(groups):
+        for r in range(1, n):
+            part_copy(g, r).wait_send()
+    send_slab(slabs - 1)
+
+    def drain(k, _):
+        wait_slab(k)
+        return 0
+
+    lax.fori_loop(max(slabs - SLOTS, 0), slabs, drain, 0)
+    own_router.wait()
+    for r in range(1, n):
+        second_copy(r).wait_recv()
+        whole = out.at[:, :, my_lanes]
+        pltpu.make_async_remote_copy(
+            src_ref=whole, dst_ref=whole,
+            send_sem=send_sem.at[0, r - 1], recv_sem=recv_sem.at[r - 1],
+            device_id={"shard": lax.rem(me + r, n)}, device_id_type=pl.DeviceIdType.MESH,
+        ).wait_recv()
+
+
+def fused(n, nz, master_gate, master_up, router_weight, router_gain):
+    experts, rows, width = master_gate.shape
+    slabs = 2 * experts
+    groups = slabs // GROUP
+    narrow = width // n
+    router_rows = router_weight.shape[1]
+    hbm = pl.BlockSpec(memory_space=pl.ANY)
+    vmem = pl.BlockSpec(memory_space=pltpu.VMEM)
+    dma = pltpu.SemaphoreType.DMA
+    out, scale, router = pl.pallas_call(
+        functools.partial(kernel, n, nz),
+        out_shape=(
+            jax.ShapeDtypeStruct((slabs, narrow, rows * n), jnp.bfloat16),
+            jax.ShapeDtypeStruct((slabs, width), jnp.float32),
+            jax.ShapeDtypeStruct((router_rows * nz, rows * n), jnp.bfloat16),
+        ),
+        in_specs=[hbm, hbm, vmem, vmem],
+        out_specs=(hbm, vmem, hbm),
+        scratch_shapes=[
+            pltpu.VMEM((slabs, rows, width), jnp.float32),
+            pltpu.VMEM((SLOTS, width, rows), jnp.bfloat16),
+            pltpu.VMEM((groups, GROUP, width), jnp.float32),
+            pltpu.VMEM((groups, n - 1, GROUP, width), jnp.float32),
+            pltpu.VMEM((width // LANES, slabs, LANES), jnp.float32),
+            pltpu.VMEM((router_rows * nz, rows), jnp.bfloat16),
+            dma((slabs,)), dma((SLOTS, n - 1)), dma((SLOTS,)), dma((n - 1,)),
+            dma((groups, n - 1)), dma((groups, n - 1)),
+            dma((nz - 1,)), dma((nz - 1,)), dma((n - 1,)), dma((n - 1,)), dma,
+        ],
+        compiler_params=pltpu.CompilerParams(
+            collective_id=0, has_side_effects=True, vmem_limit_bytes=VMEM_LIMIT),
+    )(master_gate, master_up, router_weight.T, router_gain[None, :])
+    me = lax.axis_index("shard")
+    scale = lax.dynamic_slice_in_dim(scale, me * narrow, narrow, axis=1)
+    return (
+        out[:experts].swapaxes(1, 2), out[experts:].swapaxes(1, 2),
+        scale[:experts], scale[experts:], router.T,
+    )
+
+
 def solution(mesh):
+    n, nz = mesh.shape["shard"], mesh.shape["expert"]
+
+    def local(master_gate, master_up, router_weight, router_gain):
+        experts, rows, width = master_gate.shape
+        slabs = 2 * experts
+        held = slabs * rows * width * 4 + SLOTS * rows * width * 2 + slabs * (n + 4) * width * 4
+        fits = (
+            n > 1 and nz > 1 and held <= VMEM_LIMIT and rows % LANES == 0 and width % LANES == 0
+            and width % (16 * n) == 0 and slabs % GROUP == 0 and slabs >= 2 * GROUP
+            and slabs > SLOTS and router_weight.shape[1] % 16 == 0
+        )
+        if not fits:
+            return plain(master_gate, master_up, router_weight, router_gain)
+        return fused(n, nz, master_gate, master_up, router_weight, router_gain)
+
     in_specs = (
         P("expert", "shard", None),
         P("expert", "shard", None),

time: 447 us -> 301 us (0.67)
  Pallas kernels: 0 us -> 281 us
  blocking collectives: 143 us -> 0 us
  waiting for transfers between devices: 118 us -> 0 us
  local copies, waits for them, and re-layouts: 110 us -> 18.8 us
  other arithmetic: 44.3 us -> 0 us
  starting transfers between devices: 14.6 us -> 0 us
  between operations: 14.1 us -> 0.65 us
    pallas_call x0 -> x1, Pallas kernels: none -> 281 us  [fused(): pl.pallas_call(functools.partial(kernel, n, nz), out_shape=(jax.ShapeDtyp...]
    all_gather x2 -> x0, blocking collectives: 143 us -> none  [the longest x1 131 us: local(): row_router = lax.all_gather(part_router, 'shard', axis=0, tiled=True)]
    all_to_all x2 -> x0, waiting for transfers between devices: 86 us -> none  [the longest x1 86 us: local(): lax.all_to_all(narrow_up, 'shard', split_axis=2, concat_axis=1, tiled=True)]
    all_to_all x4 -> x0, local copies, waits for them, and re-layouts: 58.6 us -> none  [the longest x2 29.3 us: local(): lax.all_to_all(narrow_gate, 'shard', split_axis=2, concat_axis=1, tiled=T...]
    unnamed x9 -> x3, local copies, waits for them, and re-layouts: 48.1 us -> 0.71 us
    psum x1 -> x0, waiting for transfers between devices: 31.6 us -> none  [local(): lax.psum((jnp.sum(master_gate * master_gate, axis=1), jnp.sum(master_up *...]
    convert_element_type x3 -> x0, other arithmetic: 28.4 us -> none  [the longest x1 14.2 us: local(): (master_up / jnp.expand_dims(scale_up, 1)).astype(jnp.bfloat16)]
    transpose x0 -> x1, local copies, waits for them, and re-layouts: none -> 16.7 us  [fused(): out[experts:].swapaxes(1, 2)]
  transfers between devices with their start and end apart: 3 -> 0, of which waited for: 2 -> 0; matrix products, arithmetic and copies ran while one was open for 17% -> 0% of each run, Pallas kernels for 0% -> 0%
where the time goes in v1:
time: 301 us
  Pallas kernels  281 us (93%)
  local copies, waits for them, and re-layouts  18.8 us (6%)
    pallas_call x1, Pallas kernels, fused(): pl.pallas_call(functools.partial(kernel, n, nz), out_shape=(jax.ShapeDtyp...  281 us
    transpose x1, local copies, waits for them, and re-layouts, fused(): out[experts:].swapaxes(1, 2)  16.7 us

profile of v1, /device:TPU:1, one launch (start us, length us, event | category | flops | bytes accessed | tf_op | source)
XLA Modules:
  0.0 300.7 jit_solution(5582569347758330464)
XLA Ops:
  0.6 281.2 %shard_map.83 = (bf16[32,176,2048]{2,1,0:T(8,128)(2,1)}, f32[32,1408]{1,0:T(8,128)}, bf16[64,2048]{1,0:T(8,128)(2,1)}) custom-call(f32[16,256,1408]{2,1,0:T(8,128)} %gate.1, f32[16,256,1408]{2,1,0:T(8,128)} %up.1, f32[16,256]{1,0:T(8,128)} %bitcast.8, f32[1,256]{1,0:T(1,128)} %bitcast.9), custom_call_target="tpu_custom_call" | custom-call | tf_op jit(solution)/shard_map/pallas_call | solution.py:231
  281.9 1.5 fusion
  283.3 0.0 copy-start
  283.3 16.7 %slice_bitcast_fusion = (bf16[16,2048,176]{1,2,0:T(8,128)(2,1)}, bf16[16,2048,176]{1,2,0:T(8,128)(2,1)}) fusion(bf16[32,176,2048]{2,1,0:T(8,128)(2,1)} %get-tuple-element.8), kind=kLoop, calls=%fused_computation | loop fusion | bytes 46137344 | tf_op jit(solution)/shard_map/transpose | solution.py:257
  300.0 0.0 copy-done
  300.0 0.7 copy.10
Async XLA Ops:
  283.3 16.7 %copy-start = (bf16[64,2048]{1,0:T(8,128)(2,1)S(1)}, bf16[64,2048]{1,0:T(8,128)(2,1)}, u32[]{:S(2)}) copy-start(bf16[64,2048]{1,0:T(8,128)(2,1)} %get-tuple-element.10) | copy-start | bytes 786436

commit v2 on v1

--- a/solution.py
+++ b/solution.py
@@ -85,6 +85,11 @@
             load(gate, 0, k).wait()
             x = buf[k]
             part[g, pl.ds(i, 1), :] = jnp.sum(x * x, axis=0, keepdims=True)
+
+            if g == 1:
+                @pl.when(i == 0)
+                def _():
+                    send_part(0)
             return 0
         lax.fori_loop(0, GROUP, one, 0)
 
@@ -154,19 +159,10 @@
 
         lax.fori_loop(0, width // LANES, tile, 0)
 
-    for g in range(groups):
-        sums(g)
-        if g == 0:
-            for r in range(1, nz):
-                first_copy(r).start()
-        else:
-            send_part(g - 1)
-        if g == 1:
-            for r in range(1, nz):
-                first_copy(r).wait()
-            for r in range(1, n):
-                second_copy(r).start()
-            own_router.start()
+    sums(0)
+    for r in range(1, nz):
+        first_copy(r).start()
+    sums(1)
 
     for g in range(groups):
         for r in range(1, n):
@@ -191,10 +187,23 @@
             if g == 0:
                 @pl.when(k == 0)
                 def _():
-                    send_part(groups - 1)
+                    send_part(1)
             return 0
 
         lax.fori_loop(0, GROUP, step, 0)
+
+        if g == 0:
+            for r in range(1, nz):
+                first_copy(r).wait()
+            for later in range(2, groups):
+                sums(later)
+                if later > 2:
+                    send_part(later - 1)
+            for r in range(1, n):
+                second_copy(r).start()
+            own_router.start()
+            if groups > 2:
+                send_part(groups - 1)
 
     for r in range(1, n):
         second_copy(r).wait_send()

time: 301 us -> 302 us (level)
  no operation moved by 1% of the time
where the time goes in v2:
time: 302 us; the launch traced here: 301 us
  Pallas kernels  282 us (93%)
  local copies, waits for them, and re-layouts  18.8 us (6%)
    pallas_call x1, Pallas kernels, fused(): pl.pallas_call(functools.partial(kernel, n, nz), out_shape=(jax.ShapeDtyp...  282 us
    transpose x1, local copies, waits for them, and re-layouts, fused(): out[experts:].swapaxes(1, 2)  16.7 us

profile of v2, /device:TPU:1, one launch (start us, length us, event | category | flops | bytes accessed | tf_op | source)
XLA Modules:
  0.0 301.4 jit_solution(12095770597630806987)
XLA Ops:
  0.6 281.9 %shard_map.83 = (bf16[32,176,2048]{2,1,0:T(8,128)(2,1)}, f32[32,1408]{1,0:T(8,128)}, bf16[64,2048]{1,0:T(8,128)(2,1)}) custom-call(f32[16,256,1408]{2,1,0:T(8,128)} %gate.1, f32[16,256,1408]{2,1,0:T(8,128)} %up.1, f32[16,256]{1,0:T(8,128)} %bitcast.8, f32[1,256]{1,0:T(1,128)} %bitcast.9), custom_call_target="tpu_custom_call" | custom-call | tf_op jit(solution)/shard_map/pallas_call | solution.py:240
  282.5 1.5 fusion
  284.0 0.0 copy-start
  284.0 16.7 %slice_bitcast_fusion = (bf16[16,2048,176]{1,2,0:T(8,128)(2,1)}, bf16[16,2048,176]{1,2,0:T(8,128)(2,1)}) fusion(bf16[32,176,2048]{2,1,0:T(8,128)(2,1)} %get-tuple-element.8), kind=kLoop, calls=%fused_computation | loop fusion | bytes 46137344 | tf_op jit(solution)/shard_map/transpose | solution.py:266
  300.7 0.0 copy-done
  300.7 0.7 copy.10
Async XLA Ops:
  284.0 16.7 %copy-start = (bf16[64,2048]{1,0:T(8,128)(2,1)S(1)}, bf16[64,2048]{1,0:T(8,128)(2,1)}, u32[]{:S(2)}) copy-start(bf16[64,2048]{1,0:T(8,128)(2,1)} %get-tuple-element.10) | copy-start | bytes 786436
